TPU v7x, 32 devices: a whole 2x2x4 slice. The times are simulated.
32 devices in a mesh: dp: 8 (over z, core), height: 4 (over y, x).
Axes of the slice: x: 2, y: 2, z: 4, core: 2. Of those that a mesh axis runs over, the one named last changes fastest.
Arguments:
- latents: bfloat16 [8, 16, 128, 640], P('dp', 'height'), parts along dimension 0, may hold values from -20 to 20
- latent_tangent: bfloat16 [8, 16, 128, 640], P('dp', 'height'), parts along dimension 0, may hold values from -20 to 20
- gain_first: float32 [640], replicated, may hold values from 0.5 to 2
- weight_first: bfloat16 [9, 640, 640], P(None, None, 'height'), may hold values from -0.078125 to 0.078125
- gain_second: float32 [640], replicated, may hold values from 0.5 to 2
- weight_second: bfloat16 [9, 640, 640], P(None, None, 'height'), may hold values from -0.078125 to 0.078125
Outputs:
- block_output: bfloat16 [8, 16, 128, 640], P('dp', 'height'), parts along dimension 0
- output_tangent: bfloat16 [8, 16, 128, 640], P('dp', 'height'), parts along dimension 0
There are 8 independent parts, one for each index of `dp`. A program takes and returns all parts, laid end to end along the dimension named above; an argument that names none is the same for every part. Nothing has to cross between parts.
All inputs are finite; a program needn't handle non-finite values.
Results may differ from a plain program's by a relative error of at most 0.006.
Values may be sent and summed in bfloat16 or wider, within the bound.
A program may use at most 128 MiB of HBM per device.

v0:
```python
import functools

import jax
import jax.numpy as jnp
import numpy as np
from jax import lax
from jax.experimental import pallas as pl
from jax.experimental.pallas import tpu as pltpu
from jax.sharding import PartitionSpec as P

GROUPS = 32
TAPS = 9
AHEAD = 6
DEPTH = 7
FAR = 2
CROSS = 6


epsilon = 1e-05
F32 = jnp.float32
BF16 = jnp.bfloat16


def fused_kernel(
    n, lat, tan, gain_a, gain_b, weight_a, weight_b, same_group,
    out, dout,
    field, mid, shifted, acc, full, stat, peer_stat,
    load_sem, halo_send, halo_recv, stat_send, stat_recv,
    own_send, near_recv, relay_send, far_recv, pair_send, pair_recv,
    plane_send, plane_recv,
):
    rows, width, chans = lat.shape[1], lat.shape[2], lat.shape[3]
    quarter = chans // n
    half = quarter // 2
    steps = 2 * TAPS
    local = rows * width
    d = lax.axis_index("dp")
    h = lax.axis_index("height")
    core = lax.rem(d, 2)
    xor1 = h + 1 - 2 * lax.rem(h, 2)
    xor2 = lax.rem(h + 2, n)
    xor3 = xor1 + 2 - 4 * (xor1 // 2)
    other = d + 1 - 2 * core
    peers = (xor1, xor2, xor3)
    plane = lax.rem(d // 2, 2)
    across = d + 2 - 4 * plane

    def start_remote(src, dst, send, recv, dd, hh):
        return pltpu.make_async_remote_copy(
            src_ref=src, dst_ref=dst, send_sem=send, recv_sem=recv,
            device_id={"dp": dd, "height": hh},
            device_id_type=pl.DeviceIdType.MESH,
        )

    barrier = pltpu.get_barrier_semaphore()
    for hh in peers:
        pl.semaphore_signal(barrier, inc=1, device_id={"dp": d, "height": hh}, device_id_type=pl.DeviceIdType.MESH)
    pl.semaphore_signal(barrier, inc=1, device_id={"dp": other, "height": h}, device_id_type=pl.DeviceIdType.MESH)

    pl.semaphore_signal(barrier, inc=1, device_id={"dp": across, "height": h}, device_id_type=pl.DeviceIdType.MESH)

    loads = [
        pltpu.make_async_copy(lat.at[0], field.at[0, pl.ds(1, rows)], load_sem.at[0]),
        pltpu.make_async_copy(tan.at[0], field.at[1, pl.ds(1, rows)], load_sem.at[1]),
    ] + [
        pltpu.make_async_copy(
            w.at[pl.ds(3 * src, 3)],
            full.at[pl.ds(TAPS * i + 3 * dst, 3), pl.ds(pl.multiple_of(h * quarter, 16), quarter)],
            load_sem.at[2 + 3 * i + dst])
        for i, w in enumerate((weight_a, weight_b)) for dst, src in enumerate((1, 0, 2))
    ]
    for c in loads:
        c.start()
    pl.semaphore_wait(barrier, n + 1)

    def rows_of(hh, cc):
        return pl.ds(pl.multiple_of(hh * quarter + cc * half, 16), half)

    def shared(s):
        return lax.rem(s, TAPS) != TAPS - 1

    def fetches(s):
        return jnp.logical_or(lax.rem(lax.rem(s, TAPS), 2) == plane, lax.rem(s, TAPS) == TAPS - 1)

    def tap_of(v):
        part = lax.rem(v, TAPS)
        row = part // 3
        return 1 - row + 3 * (row // 2), lax.rem(part, 3)

    def own_copy(s, k, w=None):
        if w is None:
            src = full.at[s, rows_of(h, core)]
        else:
            p, q = tap_of(s)
            src = w.at[3 * p + q, pl.ds(pl.multiple_of(core * half, 16), half)]
        return start_remote(
            src, full.at[s, rows_of(h, core)],
            own_send.at[s, k], near_recv.at[s, k], d, peers[k])

    def relay_copy(s):
        along = lax.rem(s, TAPS) == TAPS - 1
        source = jnp.where(along, xor2, xor1)
        target = jnp.where(along, xor1, xor2)
        block = full.at[s, rows_of(source, core)]
        return start_remote(block, block, relay_send.at[s], far_recv.at[s], d, target)

    def pair_copy(s, k):
        block = full.at[s, rows_of(peers[k], core)]
        return start_remote(block, block, pair_send.at[s, k], pair_recv.at[s, k], other, h)

    def plane_copy(s, k):
        block = full.at[s, rows_of(peers[k], core)]
        return start_remote(block, block, plane_send.at[s, k], plane_recv.at[s, k], across, h)

    def send_own(s):
        @pl.when(jnp.logical_and(fetches(s), s < TAPS))
        def _():
            for k in range(2):
                own_copy(s, k, weight_a).start()

        @pl.when(jnp.logical_and(fetches(s), s >= TAPS))
        def _():
            for k in range(2):
                own_copy(s, k, weight_b).start()

    def pass_on(s, k):
        pair_copy(s, k).start()

        @pl.when(shared(s))
        def _():
            plane_copy(s, k).start()

    def comm(s):
        @pl.when(s + AHEAD < steps)
        def _():
            send_own(s + AHEAD)

        @pl.when(jnp.logical_and(s < steps, fetches(s)))
        def _():
            for k in range(2):
                own_copy(s, k).wait_recv()
            relay_copy(s).start()
            for k in range(2):
                pass_on(s, k)

        f = s - FAR

        @pl.when(jnp.logical_and(jnp.logical_and(f >= 0, f < steps), fetches(f)))
        def _():
            relay_copy(f).wait_recv()
            pass_on(f, 2)

        z = s - CROSS

        @pl.when(jnp.logical_and(jnp.logical_and(z >= 0, z < steps), jnp.logical_not(fetches(z))))
        def _():
            for k in range(3):
                plane_copy(z, k).wait_recv()
                pair_copy(z, k).start()

    def halo_copies(buf, k):
        top = [start_remote(buf.at[f, 1], buf.at[f, rows + 1], halo_send.at[k, 0, f], halo_recv.at[k, 0, f], d, lax.rem(h + n - 1, n)) for f in range(2)]
        low = [start_remote(buf.at[f, rows], buf.at[f, 0], halo_send.at[k, 1, f], halo_recv.at[k, 1, f], d, lax.rem(h + 1, n)) for f in range(2)]
        return top, low

    def halo_start(buf, k, sources=None):
        if sources is None:
            top, low = halo_copies(buf, k)
        else:
            top = [start_remote(sources[f].at[0, 0], buf.at[f, rows + 1], halo_send.at[k, 0, f], halo_recv.at[k, 0, f], d, lax.rem(h + n - 1, n)) for f in range(2)]
            low = [start_remote(sources[f].at[0, rows - 1], buf.at[f, 0], halo_send.at[k, 1, f], halo_recv.at[k, 1, f], d, lax.rem(h + 1, n)) for f in range(2)]

        @pl.when(h > 0)
        def _():
            for c in top:
                c.start()

        @pl.when(h < n - 1)
        def _():
            for c in low:
                c.start()

    def halo_wait(buf, k):
        top, low = halo_copies(buf, k)

        @pl.when(h > 0)
        def _():
            for c in top:
                c.wait_send()
            for c in low:
                c.wait_recv()

        @pl.when(h < n - 1)
        def _():
            for c in low:
                c.wait_send()
            for c in top:
                c.wait_recv()

    def local_stats(buf, k):
        zero = jnp.zeros((1, chans), F32)

        def sums(r, carry):
            return (
                carry[0] + jnp.sum(buf[0, r].astype(F32), axis=0, keepdims=True),
                carry[1] + jnp.sum(buf[1, r].astype(F32), axis=0, keepdims=True),
            )

        total, dtotal = lax.fori_loop(1, rows + 1, sums, (zero, zero))
        mean = total / local
        dmean = dtotal / local

        def moments(r, carry):
            v = buf[0, r].astype(F32) - mean
            dv = buf[1, r].astype(F32) - dmean
            return (
                carry[0] + jnp.sum(v * v, axis=0, keepdims=True),
                carry[1] + jnp.sum(v * dv, axis=0, keepdims=True),
            )

        second, dsecond = lax.fori_loop(1, rows + 1, moments, (zero, zero))
        stat[k, 0:1] = mean
        stat[k, 1:2] = dmean
        stat[k, 2:3] = second
        stat[k, 3:4] = dsecond
        stat[k, 4:8] = jnp.zeros((4, chans), F32)

    def stat_copy(k, j):
        return start_remote(stat.at[k], peer_stat.at[k, j], stat_send.at[k, j], stat_recv.at[k, j], d, peers[j])

    def group_sum(x):
        high = x.astype(BF16)
        rest = x - high.astype(F32)
        middle = rest.astype(BF16)
        low = (rest - middle.astype(F32)).astype(BF16)
        dot = lambda part: jnp.dot(part, same_group[...], preferred_element_type=F32)
        return dot(high) + dot(middle) + dot(low)

    def coefficients(k, gain):
        gain_row = gain[...].reshape(1, chans)
        for j in range(n - 1):
            stat_copy(k, j).wait_recv()
        size = chans // GROUPS
        blocks = [stat[k]] + [peer_stat[k, j] for j in range(n - 1)]
        both = blocks[0]
        for b in blocks[1:]:
            both = both + b
        means = group_sum(both) / (n * size)
        mean, dmean = means[0:1], means[1:2]
        var = jnp.zeros((1, chans), F32)
        dvar = jnp.zeros((1, chans), F32)
        for b in blocks:
            off = b[0:1] - mean
            doff = b[1:2] - dmean
            var = var + (b[2:3] + local * (off * off))
            dvar = dvar + (b[3:4] + local * (off * doff))
        row = lax.broadcasted_iota(jnp.int32, (8, chans), 0)
        packed = jnp.where(row == 0, var, jnp.where(row == 1, dvar, 0.0))
        moments = group_sum(packed) / (n * size * local)
        inverse = lax.rsqrt(moments[0:1] + epsilon)
        scale = gain_row * inverse
        slope = gain_row * (moments[1:2] * inverse * inverse * inverse)
        return mean, dmean, scale, slope

    column = lax.broadcasted_iota(jnp.int32, (width, 1), 0)

    def activate(buf, r, coef, keep):
        mean, dmean, scale, slope = coef
        v = buf[0, r].astype(F32) - mean
        dv = buf[1, r].astype(F32) - dmean
        a = v * scale
        da = dv * scale - v * slope
        s = jax.nn.sigmoid(a)
        hid = a * s
        dhid = da * (s * (1.0 + a * (1.0 - s)))
        if keep is not None:
            hid = jnp.where(keep, hid, 0.0)
            dhid = jnp.where(keep, dhid, 0.0)
        at = pl.ds(pl.multiple_of(r * width, 128), width)
        for f, x in ((0, hid), (1, dhid)):
            shifted[1, f, at] = x.astype(BF16)
            shifted[0, f, at] = jnp.where(column == 0, 0.0, pltpu.roll(x, 1, 0)).astype(BF16)
            shifted[2, f, at] = jnp.where(column == width - 1, 0.0, pltpu.roll(x, width - 1, 0)).astype(BF16)

    def activate_rows(buf, coef):
        def one(r, carry):
            activate(buf, r, coef, None)
            return carry
        lax.fori_loop(1, rows + 1, one, 0)

    def activate_halo(buf, coef):
        def one(e, carry):
            r = e * (rows + 1)
            edge = jnp.where(e == 0, 0, n - 1)
            activate(buf, r, coef, h != edge)
            return carry
        lax.fori_loop(0, 2, one, 0)

    def multiply(v):
        pair_copy(v, 0).wait_recv()
        pair_copy(v, 1).wait_recv()
        pair_copy(v, 2).wait_recv()
        p, q = tap_of(v)

        def one(f, carry):
            acc[f] += lax.dot_general(
                shifted[q, f, pl.ds(pl.multiple_of(p * width, 128), local)], full[v],
                (((1,), (1,)), ((), ())), preferred_element_type=F32)
            return carry
        lax.fori_loop(0, 2, one, 0)

    def advance(low, high):
        def one(s, carry):
            comm(s)
            multiply(s - DEPTH)
            return carry
        lax.fori_loop(low, high, one, 0)

    for s in range(4):
        send_own(s)
    halo_start(field, 0, (lat, tan))
    for s in range(4, AHEAD):
        send_own(s)
    loads[0].wait()
    loads[1].wait()
    local_stats(field, 0)
    for j in range(n - 1):
        stat_copy(0, j).start()
    comm(0)
    comm(1)
    acc[...] = jnp.zeros_like(acc)
    coef = coefficients(0, gain_a)
    comm(2)
    activate_rows(field, coef)
    for c in loads[2:5]:
        c.wait()
    for s in range(3, DEPTH):
        comm(s)
    advance(DEPTH, DEPTH + 3)
    halo_wait(field, 0)
    activate_halo(field, coef)
    advance(DEPTH + 3, DEPTH + TAPS)
    later = DEPTH + TAPS
    for c in loads[5:]:
        c.wait()

    for f in range(2):
        for r in range(rows):
            mid[f, r + 1] = acc[f, r * width:(r + 1) * width].astype(BF16)
    halo_start(mid, 1)
    local_stats(mid, 1)
    for j in range(n - 1):
        stat_copy(1, j).start()
    comm(later + 0)
    acc[...] = jnp.zeros_like(acc)
    coef = coefficients(1, gain_b)
    comm(later + 1)
    activate_rows(mid, coef)
    comm(later + 2)
    multiply(9)
    comm(later + 3)

    def catch_up(v, carry):
        multiply(v)
        return carry
    lax.fori_loop(10, 12, catch_up, 0)
    comm(later + 4)
    halo_wait(mid, 1)
    activate_halo(mid, coef)
    comm(later + 5)
    lax.fori_loop(12, 15, catch_up, 0)
    advance(later + 6, later + TAPS)

    for f, o in ((0, out), (1, dout)):
        for r in range(rows):
            o[0, r] = (field[f, r + 1].astype(F32) + acc[f, r * width:(r + 1) * width]).astype(BF16)

    def drain(s, carry):
        @pl.when(fetches(s))
        def _():
            for k in range(2):
                own_copy(s, k).wait_send()
            relay_copy(s).wait_send()

        @pl.when(jnp.logical_and(fetches(s), shared(s)))
        def _():
            for k in range(3):
                plane_copy(s, k).wait_send()

        for k in range(3):
            pair_copy(s, k).wait_send()
        return carry
    lax.fori_loop(0, steps, drain, 0)
    for k in range(2):
        for j in range(n - 1):
            stat_copy(k, j).wait_send()


def fused(n, latents, latent_tangent, gain_first, weight_first, gain_second, weight_second):
    rows, width, chans = latents.shape[1:]
    size = chans // GROUPS
    group = np.arange(chans) // size
    same_group = jnp.asarray(group[:, None] == group[None, :], BF16)
    vmem = pl.BlockSpec(memory_space=pltpu.VMEM)
    hbm = pl.BlockSpec(memory_space=pl.ANY)
    dma = pltpu.SemaphoreType.DMA
    steps = 2 * TAPS
    shape = jax.ShapeDtypeStruct(latents.shape, BF16)
    return pl.pallas_call(
        functools.partial(fused_kernel, n),
        out_shape=(shape, shape),
        in_specs=[hbm, hbm, vmem, vmem, hbm, hbm, vmem],
        out_specs=(vmem, vmem),
        scratch_shapes=[
            pltpu.VMEM((2, rows + 2, width, chans), BF16),
            pltpu.VMEM((2, rows + 2, width, chans), BF16),
            pltpu.VMEM((3, 2, (rows + 2) * width, chans), BF16),
            pltpu.VMEM((2, rows * width, chans), F32),
            pltpu.VMEM((steps, chans, chans), BF16),
            pltpu.VMEM((2, 8, chans), F32),
            pltpu.VMEM((2, n - 1, 8, chans), F32),
            dma((8,)),
            dma((2, 2, 2)),
            dma((2, 2, 2)),
            dma((2, n - 1)),
            dma((2, n - 1)),
            dma((steps, 2)),
            dma((steps, 2)),
            dma((steps,)),
            dma((steps,)),
            dma((steps, 3)),
            dma((steps, 3)),
            dma((steps, 3)),
            dma((steps, 3)),
        ],
        compiler_params=pltpu.CompilerParams(
            collective_id=0, has_side_effects=True, vmem_limit_bytes=60 * 1024 * 1024),
    )(
        latents, latent_tangent, gain_first, gain_second,
        weight_first.transpose(0, 2, 1), weight_second.transpose(0, 2, 1), same_group)


def extended(cells, sides, width):
    for axis, dim in sides:
        count = lax.axis_size(axis)
        ends = count - 1
        head = lax.slice_in_dim(cells, 0, width, axis=dim)
        tail = lax.slice_in_dim(cells, cells.shape[dim] - width, cells.shape[dim], axis=dim)
        cells = jnp.concatenate(
            [
                lax.ppermute(tail, axis, [(i, (i + 1) % count) for i in range(ends)]),
                cells,
                lax.ppermute(head, axis, [((i + 1) % count, i) for i in range(ends)]),
            ],
            axis=dim,
        )
    return cells


def normalize(stacked, gain_vector):
    row_count, col_count, chans = (stacked.shape[1], stacked.shape[2], stacked.shape[3])
    size = chans // GROUPS
    positions = float(row_count * col_count * size * lax.axis_size("height"))
    grouped = stacked.reshape(2, row_count * col_count, GROUPS, size)
    primal = grouped[0]
    tangent = grouped[1]
    first_totals = lax.psum((jnp.sum(primal, axis=(0, 2)), jnp.sum(tangent, axis=(0, 2))), "height")
    group_mean = first_totals[0] / positions
    tangent_mean = first_totals[1] / positions
    centered = primal - group_mean[None, :, None]
    tangent_centered = tangent - tangent_mean[None, :, None]
    second_totals = lax.psum(
        (
            jnp.sum(centered * centered, axis=(0, 2)),
            jnp.sum(centered * tangent_centered, axis=(0, 2)),
        ),
        "height",
    )
    variance = second_totals[0] / positions
    dvariance = 2.0 * second_totals[1] / positions
    inverse = lax.rsqrt(variance + epsilon)[None, :, None]
    normed = centered * inverse
    dnormed = tangent_centered * inverse - centered * (0.5 * dvariance[None, :, None] * inverse**3)
    scaled = normed.reshape(row_count, col_count, chans) * gain_vector
    dscaled = dnormed.reshape(row_count, col_count, chans) * gain_vector
    sigmoid_value = jax.nn.sigmoid(scaled)
    hidden = scaled * sigmoid_value
    dhidden = dscaled * sigmoid_value * (1.0 + scaled * (1.0 - sigmoid_value))
    return jnp.stack([hidden, dhidden], 0).astype(jnp.bfloat16)


def apply_taps(padded, weight_piece, row_count, col_count):
    chans = padded.shape[3]
    accumulated = jnp.zeros((2 * row_count * col_count, weight_piece.shape[2]), jnp.float32)
    for tap_index in range(9):
        offset_row = tap_index // 3
        offset_col = tap_index % 3
        window = padded[
            :, offset_row : offset_row + row_count, offset_col : offset_col + col_count, :
        ].reshape(-1, chans)
        accumulated = accumulated + jnp.dot(
            window, weight_piece[tap_index], preferred_element_type=jnp.float32
        )
    return accumulated


def convolve(hidden, weight):
    row_count, col_count = (hidden.shape[1], hidden.shape[2])
    padded = extended(hidden, (("height", 1),), 1)
    padded = jnp.pad(padded, ((0, 0), (0, 0), (1, 1), (0, 0)))
    flattened = apply_taps(
        padded, lax.all_gather(weight, "height", axis=2, tiled=True), row_count, col_count
    )
    return flattened.reshape(2, row_count, col_count, -1)


def per_device(latents, latent_tangent, gain_first, weight_first, gain_second, weight_second):
    stacked = jnp.concatenate([latents, latent_tangent], 0).astype(jnp.float32)
    hidden = normalize(stacked, gain_first)
    middle = convolve(hidden, weight_first).astype(jnp.bfloat16)
    second = normalize(middle.astype(jnp.float32), gain_second)
    result = (stacked + convolve(second, weight_second)).astype(jnp.bfloat16)
    return (result[0:1], result[1:2])


def solution(mesh):
    placed = (
        P("dp", "height", None, None),
        P("dp", "height", None, None),
        P(),
        P(None, None, "height"),
        P(),
        P(None, None, "height"),
    )
    n = mesh.shape["height"]
    body = per_device
    if n == 4 and mesh.shape["dp"] % 4 == 0:
        body = functools.partial(fused, n)
    return jax.shard_map(
        body,
        mesh=mesh,
        in_specs=placed,
        out_specs=(P("dp", "height", None, None), P("dp", "height", None, None)),
        check_vma=False,
    )
```

profile of v0, /device:TPU:24, one launch (start us, length us, event | category | flops | bytes accessed | tf_op | source)
XLA Modules:
  0.0 107.6 jit_solution(13987231743770076399)
XLA Ops:
  0.6 103.0 %shard_map.86 = (bf16[1,4,128,640]{3,2,1,0:T(8,128)(2,1)}, bf16[1,4,128,640]{3,2,1,0:T(8,128)(2,1)}) custom-call(bf16[1,4,128,640]{3,2,1,0:T(8,128)(2,1)} %lat.1, bf16[1,4,128,640]{3,2,1,0:T(8,128)(2,1)} %tan.1, f32[640]{0:T(1024)} %gain_a.1, f32[640]{0:T(1024)} %gain_b.1, bf16[9,160,640]{2,1,0:T(8,128)(2,1)} %bitcast.2, bf16[9,160,640]{2,1,0:T(8,128)(2,1)} %bitcast.3, ...), custom_call_target="tpu_custom_call" | custom-call | tf_op jit(solution)/shard_map/pallas_call | solution.py:409
  103.6 2.0 %copy.11 = bf16[1,4,128,640]{3,2,1,0:T(8,128)(2,1)} copy(bf16[1,4,128,640]{3,2,1,0:T(8,128)(2,1)} %get-tuple-element.4) | data formatting | bytes 1310720
  105.6 2.0 %copy.12 = bf16[1,4,128,640]{3,2,1,0:T(8,128)(2,1)} copy(bf16[1,4,128,640]{3,2,1,0:T(8,128)(2,1)} %get-tuple-element.5) | data formatting | bytes 1310720
where the time goes:
time: 108 us
  Pallas kernels  103 us (95%)
  local copies, waits for them, and re-layouts  3.96 us (4%)
    pallas_call x1, Pallas kernels, fused(): pl.pallas_call(functools.partial(fused_kernel, n), out_shape=(shape, shap...  103 us
    unnamed x2, local copies, waits for them, and re-layouts  3.96 us

commit v1 on v0

--- a/solution.py
+++ b/solution.py
@@ -11,9 +11,9 @@
 GROUPS = 32
 TAPS = 9
 AHEAD = 6
-DEPTH = 7
 FAR = 2
 CROSS = 6
+DOUBLE = 15
 
 
 epsilon = 1e-05
@@ -34,6 +34,7 @@
     half = quarter // 2
     steps = 2 * TAPS
     local = rows * width
+    pair = 2 * width
     d = lax.axis_index("dp")
     h = lax.axis_index("height")
     core = lax.rem(d, 2)
@@ -71,16 +72,14 @@
     ]
     for c in loads:
         c.start()
-    pl.semaphore_wait(barrier, n + 1)
-
     def rows_of(hh, cc):
         return pl.ds(pl.multiple_of(hh * quarter + cc * half, 16), half)
 
     def shared(s):
-        return lax.rem(s, TAPS) != TAPS - 1
+        return jnp.logical_and(lax.rem(s, TAPS) != TAPS - 1, s < DOUBLE)
 
     def fetches(s):
-        return jnp.logical_or(lax.rem(lax.rem(s, TAPS), 2) == plane, lax.rem(s, TAPS) == TAPS - 1)
+        return jnp.logical_or(lax.rem(lax.rem(s, TAPS), 2) == plane, jnp.logical_not(shared(s)))
 
     def tap_of(v):
         part = lax.rem(v, TAPS)
@@ -98,7 +97,7 @@
             own_send.at[s, k], near_recv.at[s, k], d, peers[k])
 
     def relay_copy(s):
-        along = lax.rem(s, TAPS) == TAPS - 1
+        along = jnp.logical_and(lax.rem(lax.rem(s, TAPS) // 2, 2) == 1, jnp.logical_or(h == 0, h == n - 1))
         source = jnp.where(along, xor2, xor1)
         target = jnp.where(along, xor1, xor2)
         block = full.at[s, rows_of(source, core)]
@@ -163,22 +162,19 @@
         low = [start_remote(buf.at[f, rows], buf.at[f, 0], halo_send.at[k, 1, f], halo_recv.at[k, 1, f], d, lax.rem(h + 1, n)) for f in range(2)]
         return top, low
 
-    def halo_start(buf, k, sources=None):
-        if sources is None:
-            top, low = halo_copies(buf, k)
-        else:
-            top = [start_remote(sources[f].at[0, 0], buf.at[f, rows + 1], halo_send.at[k, 0, f], halo_recv.at[k, 0, f], d, lax.rem(h + n - 1, n)) for f in range(2)]
-            low = [start_remote(sources[f].at[0, rows - 1], buf.at[f, 0], halo_send.at[k, 1, f], halo_recv.at[k, 1, f], d, lax.rem(h + 1, n)) for f in range(2)]
+    def halo_start(buf, k, sources=None, fields=(0, 1)):
+        def edge_row(f, r):
+            return buf.at[f, 1 + r] if sources is None else sources[f].at[0, r]
 
         @pl.when(h > 0)
         def _():
-            for c in top:
-                c.start()
+            for f in fields:
+                start_remote(edge_row(f, 0), buf.at[f, rows + 1], halo_send.at[k, 0, f], halo_recv.at[k, 0, f], d, lax.rem(h + n - 1, n)).start()
 
         @pl.when(h < n - 1)
         def _():
-            for c in low:
-                c.start()
+            for f in fields:
+                start_remote(edge_row(f, rows - 1), buf.at[f, 0], halo_send.at[k, 1, f], halo_recv.at[k, 1, f], d, lax.rem(h + 1, n)).start()
 
     def halo_wait(buf, k):
         top, low = halo_copies(buf, k)
@@ -276,11 +272,11 @@
         if keep is not None:
             hid = jnp.where(keep, hid, 0.0)
             dhid = jnp.where(keep, dhid, 0.0)
-        at = pl.ds(pl.multiple_of(r * width, 128), width)
         for f, x in ((0, hid), (1, dhid)):
-            shifted[1, f, at] = x.astype(BF16)
-            shifted[0, f, at] = jnp.where(column == 0, 0.0, pltpu.roll(x, 1, 0)).astype(BF16)
-            shifted[2, f, at] = jnp.where(column == width - 1, 0.0, pltpu.roll(x, width - 1, 0)).astype(BF16)
+            at = pl.ds(pl.multiple_of(r * pair + f * width, 128), width)
+            shifted[1, at] = x.astype(BF16)
+            shifted[0, at] = jnp.where(column == 0, 0.0, pltpu.roll(x, 1, 0)).astype(BF16)
+            shifted[2, at] = jnp.where(column == width - 1, 0.0, pltpu.roll(x, width - 1, 0)).astype(BF16)
 
     def activate_rows(buf, coef):
         def one(r, carry):
@@ -296,84 +292,92 @@
             return carry
         lax.fori_loop(0, 2, one, 0)
 
-    def multiply(v):
-        pair_copy(v, 0).wait_recv()
-        pair_copy(v, 1).wait_recv()
-        pair_copy(v, 2).wait_recv()
-        p, q = tap_of(v)
-
-        def one(f, carry):
-            acc[f] += lax.dot_general(
-                shifted[q, f, pl.ds(pl.multiple_of(p * width, 128), local)], full[v],
-                (((1,), (1,)), ((), ())), preferred_element_type=F32)
-            return carry
-        lax.fori_loop(0, 2, one, 0)
-
-    def advance(low, high):
-        def one(s, carry):
-            comm(s)
-            multiply(s - DEPTH)
+    def arrive(v):
+        for k in range(3):
+            pair_copy(v, k).wait_recv()
+
+    def accumulate(v, src, dst, count):
+        q = tap_of(v)[1]
+        at = pl.ds(pl.multiple_of(dst * pair, 128), count * pair)
+        acc[at] += lax.dot_general(
+            shifted[q, pl.ds(pl.multiple_of(src * pair, 128), count * pair)], full[v],
+            (((1,), (1,)), ((), ())), preferred_element_type=F32)
+
+    def loop(low, high, body):
+        def one(v, carry):
+            body(v)
             return carry
         lax.fori_loop(low, high, one, 0)
 
-    for s in range(4):
-        send_own(s)
-    halo_start(field, 0, (lat, tan))
-    for s in range(4, AHEAD):
-        send_own(s)
+    def center(v):
+        comm(v + CROSS + 1)
+        arrive(v)
+        accumulate(v, 1, 0, rows)
+
+    def inner(v):
+        comm(v + CROSS + 1)
+        arrive(v)
+        p = tap_of(v)[0]
+        accumulate(v, 1 + p // 2, 1 - p // 2, rows - 1)
+
+    def edge(v):
+        p = tap_of(v)[0]
+        accumulate(v, (p // 2) * (rows + 1), (p // 2) * (rows - 1), 1)
+
     loads[0].wait()
     loads[1].wait()
     local_stats(field, 0)
+    pl.semaphore_wait(barrier, n + 1)
     for j in range(n - 1):
         stat_copy(0, j).start()
+    for s in range(4):
+        send_own(s)
+    halo_start(field, 0, (lat, tan), (0,))
+    for s in range(4, AHEAD):
+        send_own(s)
     comm(0)
     comm(1)
+    halo_start(field, 0, (lat, tan), (1,))
     acc[...] = jnp.zeros_like(acc)
     coef = coefficients(0, gain_a)
     comm(2)
     activate_rows(field, coef)
     for c in loads[2:5]:
         c.wait()
-    for s in range(3, DEPTH):
+    for s in range(3, CROSS + 1):
         comm(s)
-    advance(DEPTH, DEPTH + 3)
+    loop(0, 3, center)
+    loop(3, TAPS, inner)
     halo_wait(field, 0)
     activate_halo(field, coef)
-    advance(DEPTH + 3, DEPTH + TAPS)
-    later = DEPTH + TAPS
+    loop(3, TAPS, edge)
+
     for c in loads[5:]:
         c.wait()
-
     for f in range(2):
         for r in range(rows):
-            mid[f, r + 1] = acc[f, r * width:(r + 1) * width].astype(BF16)
-    halo_start(mid, 1)
+            at = r * pair + f * width
+            mid[f, r + 1] = acc[at:at + width].astype(BF16)
     local_stats(mid, 1)
     for j in range(n - 1):
         stat_copy(1, j).start()
-    comm(later + 0)
+    halo_start(mid, 1)
     acc[...] = jnp.zeros_like(acc)
     coef = coefficients(1, gain_b)
-    comm(later + 1)
     activate_rows(mid, coef)
-    comm(later + 2)
-    multiply(9)
-    comm(later + 3)
-
-    def catch_up(v, carry):
-        multiply(v)
-        return carry
-    lax.fori_loop(10, 12, catch_up, 0)
-    comm(later + 4)
+    loop(TAPS, TAPS + 3, center)
+    loop(TAPS + 3, steps - 1, inner)
     halo_wait(mid, 1)
     activate_halo(mid, coef)
-    comm(later + 5)
-    lax.fori_loop(12, 15, catch_up, 0)
-    advance(later + 6, later + TAPS)
+    loop(TAPS + 3, steps - 1, edge)
+    comm(steps + CROSS)
+    arrive(steps - 1)
+    accumulate(steps - 1, 2, 0, rows)
 
     for f, o in ((0, out), (1, dout)):
         for r in range(rows):
-            o[0, r] = (field[f, r + 1].astype(F32) + acc[f, r * width:(r + 1) * width]).astype(BF16)
+            at = r * pair + f * width
+            o[0, r] = (field[f, r + 1].astype(F32) + acc[at:at + width]).astype(BF16)
 
     def drain(s, carry):
         @pl.when(fetches(s))
@@ -414,8 +418,8 @@
         scratch_shapes=[
             pltpu.VMEM((2, rows + 2, width, chans), BF16),
             pltpu.VMEM((2, rows + 2, width, chans), BF16),
-            pltpu.VMEM((3, 2, (rows + 2) * width, chans), BF16),
-            pltpu.VMEM((2, rows * width, chans), F32),
+            pltpu.VMEM((3, (rows + 2) * 2 * width, chans), BF16),
+            pltpu.VMEM((2 * rows * width, chans), F32),
             pltpu.VMEM((steps, chans, chans), BF16),
             pltpu.VMEM((2, 8, chans), F32),
             pltpu.VMEM((2, n - 1, 8, chans), F32),

time: 108 us -> 93.8 us (0.87)
  the two profiles are of different devices: /device:TPU:24 before, /device:TPU:3 now
where the time goes in v1:
time: 93.8 us; the launch traced here: 92 us
  Pallas kernels  87.4 us (93%)
  local copies, waits for them, and re-layouts  3.96 us (4%)
    pallas_call x1, Pallas kernels, fused(): pl.pallas_call(functools.partial(fused_kernel, n), out_shape=(shape, shap...  87.4 us
    unnamed x2, local copies, waits for them, and re-layouts  3.96 us

profile of v1, /device:TPU:3, one launch (start us, length us, event | category | flops | bytes accessed | tf_op | source)
XLA Modules:
  0.0 92.0 jit_solution(3340955807351527785)
XLA Ops:
  0.6 87.4 %shard_map.86 = (bf16[1,4,128,640]{3,2,1,0:T(8,128)(2,1)}, bf16[1,4,128,640]{3,2,1,0:T(8,128)(2,1)}) custom-call(bf16[1,4,128,640]{3,2,1,0:T(8,128)(2,1)} %lat.1, bf16[1,4,128,640]{3,2,1,0:T(8,128)(2,1)} %tan.1, f32[640]{0:T(1024)} %gain_a.1, f32[640]{0:T(1024)} %gain_b.1, bf16[9,160,640]{2,1,0:T(8,128)(2,1)} %bitcast.2, bf16[9,160,640]{2,1,0:T(8,128)(2,1)} %bitcast.3, ...), custom_call_target="tpu_custom_call" | custom-call | tf_op jit(solution)/shard_map/pallas_call | solution.py:413
  88.1 2.0 %copy.11 = bf16[1,4,128,640]{3,2,1,0:T(8,128)(2,1)} copy(bf16[1,4,128,640]{3,2,1,0:T(8,128)(2,1)} %get-tuple-element.4) | data formatting | bytes 1310720
  90.1 2.0 %copy.12 = bf16[1,4,128,640]{3,2,1,0:T(8,128)(2,1)} copy(bf16[1,4,128,640]{3,2,1,0:T(8,128)(2,1)} %get-tuple-element.5) | data formatting | bytes 1310720

commit v2 on v1

--- a/solution.py
+++ b/solution.py
@@ -10,11 +10,13 @@
 
 GROUPS = 32
 TAPS = 9
-AHEAD = 6
-FAR = 2
-CROSS = 6
+ALONE = 8
 DOUBLE = 15
-
+FIRST = 4
+OWN = (7, 9, 12, 12, 14, 14, 14, 15, 16, 17, 17, 18, 18, 18, 18, 18, 18, 18, 18, 18, 18, 18, 18)
+NEAR = (2, 5, 7, 9, 10, 10, 12, 12, 13, 13, 14, 15, 17, 17, 17, 17, 18, 18, 18, 18, 18, 18, 18)
+LATE = (0, 2, 3, 7, 7, 9, 9, 10, 10, 10, 10, 10, 12, 14, 14, 15, 15, 16, 16, 17, 18, 18, 18)
+CROSS = (0, 0, 1, 2, 3, 6, 6, 8, 8, 9, 9, 9, 10, 12, 12, 12, 14, 16, 16, 17, 17, 17, 18)
 
 epsilon = 1e-05
 F32 = jnp.float32
@@ -76,32 +78,33 @@
         return pl.ds(pl.multiple_of(hh * quarter + cc * half, 16), half)
 
     def shared(s):
-        return jnp.logical_and(lax.rem(s, TAPS) != TAPS - 1, s < DOUBLE)
-
-    def fetches(s):
-        return jnp.logical_or(lax.rem(lax.rem(s, TAPS), 2) == plane, jnp.logical_not(shared(s)))
+        return s < ALONE or TAPS <= s < DOUBLE
+
+    def fetched(s, side):
+        return not shared(s) or s % TAPS % 2 == side
+
+    corner = jnp.logical_or(h == 0, h == n - 1)
+    turn_source = jnp.where(corner, xor2, xor1)
+    turn_target = jnp.where(corner, xor1, xor2)
 
     def tap_of(v):
         part = lax.rem(v, TAPS)
         row = part // 3
         return 1 - row + 3 * (row // 2), lax.rem(part, 3)
 
-    def own_copy(s, k, w=None):
+    def own_copy(s, k, w=None, tap=None):
         if w is None:
             src = full.at[s, rows_of(h, core)]
         else:
-            p, q = tap_of(s)
-            src = w.at[3 * p + q, pl.ds(pl.multiple_of(core * half, 16), half)]
+            src = w.at[tap, pl.ds(pl.multiple_of(core * half, 16), half)]
         return start_remote(
             src, full.at[s, rows_of(h, core)],
             own_send.at[s, k], near_recv.at[s, k], d, peers[k])
 
     def relay_copy(s):
-        along = jnp.logical_and(lax.rem(lax.rem(s, TAPS) // 2, 2) == 1, jnp.logical_or(h == 0, h == n - 1))
-        source = jnp.where(along, xor2, xor1)
-        target = jnp.where(along, xor1, xor2)
-        block = full.at[s, rows_of(source, core)]
-        return start_remote(block, block, relay_send.at[s], far_recv.at[s], d, target)
+        turn = s % TAPS // 2 % 2 == 1
+        block = full.at[s, rows_of(turn_source if turn else xor1, core)]
+        return start_remote(block, block, relay_send.at[s], far_recv.at[s], d, turn_target if turn else xor2)
 
     def pair_copy(s, k):
         block = full.at[s, rows_of(peers[k], core)]
@@ -111,51 +114,62 @@
         block = full.at[s, rows_of(peers[k], core)]
         return start_remote(block, block, plane_send.at[s, k], plane_recv.at[s, k], across, h)
 
-    def send_own(s):
-        @pl.when(jnp.logical_and(fetches(s), s < TAPS))
-        def _():
+    def send_own(s, side):
+        if fetched(s, side):
+            p, q = (1, 0, 2)[s % TAPS // 3], s % 3
             for k in range(2):
-                own_copy(s, k, weight_a).start()
-
-        @pl.when(jnp.logical_and(fetches(s), s >= TAPS))
-        def _():
-            for k in range(2):
-                own_copy(s, k, weight_b).start()
+                own_copy(s, k, (weight_a, weight_b)[s // TAPS], 3 * p + q).start()
 
     def pass_on(s, k):
         pair_copy(s, k).start()
-
-        @pl.when(shared(s))
-        def _():
+        if shared(s):
             plane_copy(s, k).start()
 
-    def comm(s):
-        @pl.when(s + AHEAD < steps)
-        def _():
-            send_own(s + AHEAD)
-
-        @pl.when(jnp.logical_and(s < steps, fetches(s)))
-        def _():
+    def relay(s, side):
+        if fetched(s, side):
             for k in range(2):
                 own_copy(s, k).wait_recv()
             relay_copy(s).start()
             for k in range(2):
                 pass_on(s, k)
 
-        f = s - FAR
-
-        @pl.when(jnp.logical_and(jnp.logical_and(f >= 0, f < steps), fetches(f)))
-        def _():
-            relay_copy(f).wait_recv()
-            pass_on(f, 2)
-
-        z = s - CROSS
-
-        @pl.when(jnp.logical_and(jnp.logical_and(z >= 0, z < steps), jnp.logical_not(fetches(z))))
-        def _():
+    def spread(s, side):
+        if fetched(s, side):
+            relay_copy(s).wait_recv()
+            pass_on(s, 2)
+
+    def mirror(s, side):
+        if not fetched(s, side):
             for k in range(3):
-                plane_copy(z, k).wait_recv()
-                pair_copy(z, k).start()
+                plane_copy(s, k).wait_recv()
+                pair_copy(s, k).start()
+
+    def both_planes(work):
+        for side in range(2):
+            @pl.when(plane == side)
+            def _(side=side):
+                for action, s in work:
+                    action(s, side)
+
+    def tick(t):
+        work = []
+        for action, table in ((spread, LATE), (mirror, CROSS), (relay, NEAR), (send_own, OWN)):
+            before = table[t - 1] if t else FIRST if table is OWN else 0
+            work += [(action, s) for s in range(before, table[t])]
+        if work:
+            both_planes(work)
+
+    def loop(low, high, body):
+        def one(v, carry):
+            body(v)
+            return carry
+        lax.fori_loop(low, high, one, 0)
+
+    def ticks(v, low, high, offset):
+        for u in range(low, high):
+            @pl.when(v == u)
+            def _(u=u):
+                tick(u + offset)
 
     def halo_copies(buf, k):
         top = [start_remote(buf.at[f, 1], buf.at[f, rows + 1], halo_send.at[k, 0, f], halo_recv.at[k, 0, f], d, lax.rem(h + n - 1, n)) for f in range(2)]
@@ -303,22 +317,20 @@
             shifted[q, pl.ds(pl.multiple_of(src * pair, 128), count * pair)], full[v],
             (((1,), (1,)), ((), ())), preferred_element_type=F32)
 
-    def loop(low, high, body):
-        def one(v, carry):
-            body(v)
-            return carry
-        lax.fori_loop(low, high, one, 0)
-
-    def center(v):
-        comm(v + CROSS + 1)
-        arrive(v)
-        accumulate(v, 1, 0, rows)
-
-    def inner(v):
-        comm(v + CROSS + 1)
-        arrive(v)
-        p = tap_of(v)[0]
-        accumulate(v, 1 + p // 2, 1 - p // 2, rows - 1)
+    def center(low, high, offset):
+        def one(v):
+            ticks(v, low, high, offset)
+            arrive(v)
+            accumulate(v, 1, 0, rows)
+        loop(low, high, one)
+
+    def inner(low, high, offset):
+        def one(v):
+            ticks(v, low, high, offset)
+            arrive(v)
+            p = tap_of(v)[0]
+            accumulate(v, 1 + p // 2, 1 - p // 2, rows - 1)
+        loop(low, high, one)
 
     def edge(v):
         p = tap_of(v)[0]
@@ -330,24 +342,20 @@
     pl.semaphore_wait(barrier, n + 1)
     for j in range(n - 1):
         stat_copy(0, j).start()
-    for s in range(4):
-        send_own(s)
+    both_planes([(send_own, s) for s in range(FIRST)])
+    tick(0)
     halo_start(field, 0, (lat, tan), (0,))
-    for s in range(4, AHEAD):
-        send_own(s)
-    comm(0)
-    comm(1)
-    halo_start(field, 0, (lat, tan), (1,))
     acc[...] = jnp.zeros_like(acc)
     coef = coefficients(0, gain_a)
-    comm(2)
+    tick(1)
     activate_rows(field, coef)
     for c in loads[2:5]:
         c.wait()
-    for s in range(3, CROSS + 1):
-        comm(s)
-    loop(0, 3, center)
-    loop(3, TAPS, inner)
+    center(0, 2, 2)
+    halo_start(field, 0, (lat, tan), (1,))
+    center(2, 3, 2)
+    inner(3, 9, 2)
+    tick(11)
     halo_wait(field, 0)
     activate_halo(field, coef)
     loop(3, TAPS, edge)
@@ -362,15 +370,17 @@
     for j in range(n - 1):
         stat_copy(1, j).start()
     halo_start(mid, 1)
+    tick(12)
     acc[...] = jnp.zeros_like(acc)
     coef = coefficients(1, gain_b)
+    tick(13)
     activate_rows(mid, coef)
-    loop(TAPS, TAPS + 3, center)
-    loop(TAPS + 3, steps - 1, inner)
+    center(TAPS, TAPS + 3, 5)
+    inner(TAPS + 3, 17, 5)
     halo_wait(mid, 1)
     activate_halo(mid, coef)
-    loop(TAPS + 3, steps - 1, edge)
-    comm(steps + CROSS)
+    loop(TAPS + 3, 17, edge)
+    tick(22)
     arrive(steps - 1)
     accumulate(steps - 1, 2, 0, rows)
 
@@ -379,22 +389,17 @@
             at = r * pair + f * width
             o[0, r] = (field[f, r + 1].astype(F32) + acc[at:at + width]).astype(BF16)
 
-    def drain(s, carry):
-        @pl.when(fetches(s))
-        def _():
+    def drain(s, side):
+        if fetched(s, side):
             for k in range(2):
                 own_copy(s, k).wait_send()
             relay_copy(s).wait_send()
-
-        @pl.when(jnp.logical_and(fetches(s), shared(s)))
-        def _():
-            for k in range(3):
-                plane_copy(s, k).wait_send()
-
+            if shared(s):
+                for k in range(3):
+                    plane_copy(s, k).wait_send()
         for k in range(3):
             pair_copy(s, k).wait_send()
-        return carry
-    lax.fori_loop(0, steps, drain, 0)
+    both_planes([(drain, s) for s in range(steps)])
     for k in range(2):
         for j in range(n - 1):
             stat_copy(k, j).wait_send()

time: 93.8 us -> 86.7 us (0.924)
  Pallas kernels: 87.4 us -> 81.2 us
    pallas_call x1, Pallas kernels: 87.4 us -> 81.2 us  [fused(): pl.pallas_call(functools.partial(fused_kernel, n), out_shape=(shape, shap...]
where the time goes in v2:
time: 86.7 us; the launch traced here: 85.8 us
  Pallas kernels  81.2 us (94%)
  local copies, waits for them, and re-layouts  3.96 us (5%)
    pallas_call x1, Pallas kernels, fused(): pl.pallas_call(functools.partial(fused_kernel, n), out_shape=(shape, shap...  81.2 us
    unnamed x2, local copies, waits for them, and re-layouts  3.96 us

profile of v2, /device:TPU:3, one launch (start us, length us, event | category | flops | bytes accessed | tf_op | source)
XLA Modules:
  0.0 85.8 jit_solution(9074523614516952092)
XLA Ops:
  0.6 81.2 %shard_map.86 = (bf16[1,4,128,640]{3,2,1,0:T(8,128)(2,1)}, bf16[1,4,128,640]{3,2,1,0:T(8,128)(2,1)}) custom-call(bf16[1,4,128,640]{3,2,1,0:T(8,128)(2,1)} %lat.1, bf16[1,4,128,640]{3,2,1,0:T(8,128)(2,1)} %tan.1, f32[640]{0:T(1024)} %gain_a.1, f32[640]{0:T(1024)} %gain_b.1, bf16[9,160,640]{2,1,0:T(8,128)(2,1)} %bitcast.2, bf16[9,160,640]{2,1,0:T(8,128)(2,1)} %bitcast.3, ...), custom_call_target="tpu_custom_call" | custom-call | tf_op jit(solution)/shard_map/pallas_call | solution.py:418
  81.8 2.0 %copy.11 = bf16[1,4,128,640]{3,2,1,0:T(8,128)(2,1)} copy(bf16[1,4,128,640]{3,2,1,0:T(8,128)(2,1)} %get-tuple-element.4) | data formatting | bytes 1310720
  83.8 2.0 %copy.12 = bf16[1,4,128,640]{3,2,1,0:T(8,128)(2,1)} copy(bf16[1,4,128,640]{3,2,1,0:T(8,128)(2,1)} %get-tuple-element.5) | data formatting | bytes 1310720

commit v3 on v2

--- a/solution.py
+++ b/solution.py
@@ -10,13 +10,14 @@
 
 GROUPS = 32
 TAPS = 9
-ALONE = 8
-DOUBLE = 15
-FIRST = 4
-OWN = (7, 9, 12, 12, 14, 14, 14, 15, 16, 17, 17, 18, 18, 18, 18, 18, 18, 18, 18, 18, 18, 18, 18)
-NEAR = (2, 5, 7, 9, 10, 10, 12, 12, 13, 13, 14, 15, 17, 17, 17, 17, 18, 18, 18, 18, 18, 18, 18)
-LATE = (0, 2, 3, 7, 7, 9, 9, 10, 10, 10, 10, 10, 12, 14, 14, 15, 15, 16, 16, 17, 18, 18, 18)
-CROSS = (0, 0, 1, 2, 3, 6, 6, 8, 8, 9, 9, 9, 10, 12, 12, 12, 14, 16, 16, 17, 17, 17, 18)
+SHARED = (1, 1, 1, 0, 1, 1, 1, 0, 1, 1, 1, 1, 1, 1, 0, 1, 1, 0)
+SIDE = (0, 0, 1, 0, 1, 0, 1, 0, 1, 0, 0, 1, 0, 1, 1, 1, 0, 1)
+TURN = (1, 0, 1, 1, 0, 1, 0, 0, 1, 0, 1, 1, 1, 1, 1, 1, 1, 1)
+FIRST = 7
+OWN = (10, 11, 13, 14, 14, 14, 14, 14, 16, 18, 18, 18, 18, 18, 18, 18, 18, 18, 18, 18, 18, 18, 18)
+NEAR = (2, 7, 9, 9, 11, 11, 11, 12, 12, 12, 12, 14, 18, 18, 18, 18, 18, 18, 18, 18, 18, 18, 18)
+LATE = (0, 2, 4, 5, 7, 8, 9, 9, 9, 9, 10, 11, 14, 14, 14, 15, 17, 17, 17, 17, 18, 18, 18)
+CROSS = (0, 0, 1, 4, 4, 5, 5, 7, 9, 9, 9, 9, 10, 11, 12, 14, 14, 15, 15, 18, 18, 18, 18)
 
 epsilon = 1e-05
 F32 = jnp.float32
@@ -78,10 +79,10 @@
         return pl.ds(pl.multiple_of(hh * quarter + cc * half, 16), half)
 
     def shared(s):
-        return s < ALONE or TAPS <= s < DOUBLE
+        return SHARED[s] == 1
 
     def fetched(s, side):
-        return not shared(s) or s % TAPS % 2 == side
+        return not shared(s) or SIDE[s] == side
 
     corner = jnp.logical_or(h == 0, h == n - 1)
     turn_source = jnp.where(corner, xor2, xor1)
@@ -102,7 +103,7 @@
             own_send.at[s, k], near_recv.at[s, k], d, peers[k])
 
     def relay_copy(s):
-        turn = s % TAPS // 2 % 2 == 1
+        turn = TURN[s] == 1
         block = full.at[s, rows_of(turn_source if turn else xor1, core)]
         return start_remote(block, block, relay_send.at[s], far_recv.at[s], d, turn_target if turn else xor2)
 
@@ -153,7 +154,7 @@
 
     def tick(t):
         work = []
-        for action, table in ((spread, LATE), (mirror, CROSS), (relay, NEAR), (send_own, OWN)):
+        for action, table in ((mirror, CROSS), (spread, LATE), (relay, NEAR), (send_own, OWN)):
             before = table[t - 1] if t else FIRST if table is OWN else 0
             work += [(action, s) for s in range(before, table[t])]
         if work:
@@ -344,16 +345,16 @@
         stat_copy(0, j).start()
     both_planes([(send_own, s) for s in range(FIRST)])
     tick(0)
-    halo_start(field, 0, (lat, tan), (0,))
     acc[...] = jnp.zeros_like(acc)
     coef = coefficients(0, gain_a)
     tick(1)
+    halo_start(field, 0, (lat, tan), (0,))
     activate_rows(field, coef)
     for c in loads[2:5]:
         c.wait()
-    center(0, 2, 2)
+    center(0, 1, 2)
     halo_start(field, 0, (lat, tan), (1,))
-    center(2, 3, 2)
+    center(1, 3, 2)
     inner(3, 9, 2)
     tick(11)
     halo_wait(field, 0)
@@ -369,11 +370,12 @@
     local_stats(mid, 1)
     for j in range(n - 1):
         stat_copy(1, j).start()
-    halo_start(mid, 1)
     tick(12)
+    halo_start(mid, 1, None, (0,))
     acc[...] = jnp.zeros_like(acc)
     coef = coefficients(1, gain_b)
     tick(13)
+    halo_start(mid, 1, None, (1,))
     activate_rows(mid, coef)
     center(TAPS, TAPS + 3, 5)
     inner(TAPS + 3, 17, 5)
@@ -417,7 +419,7 @@
     shape = jax.ShapeDtypeStruct(latents.shape, BF16)
     return pl.pallas_call(
         functools.partial(fused_kernel, n),
-        out_shape=(shape, shape),
+        out_shape=(pltpu.VMEM(latents.shape, BF16), pltpu.VMEM(latents.shape, BF16)),
         in_specs=[hbm, hbm, vmem, vmem, hbm, hbm, vmem],
         out_specs=(vmem, vmem),
         scratch_shapes=[
@@ -443,7 +445,7 @@
             dma((steps, 3)),
         ],
         compiler_params=pltpu.CompilerParams(
-            collective_id=0, has_side_effects=True, vmem_limit_bytes=60 * 1024 * 1024),
+            collective_id=0, has_side_effects=True, vmem_limit_bytes=61 * 1024 * 1024),
     )(
         latents, latent_tangent, gain_first, gain_second,
         weight_first.transpose(0, 2, 1), weight_second.transpose(0, 2, 1), same_group)

time: 86.7 us -> 75.4 us (0.87)
  Pallas kernels: 81.2 us -> 72.6 us
  local copies, waits for them, and re-layouts: 3.96 us -> 1.67 us
    pallas_call x1, Pallas kernels: 81.2 us -> 72.6 us  [fused(): pl.pallas_call(functools.partial(fused_kernel, n), out_shape=(pltpu.VMEM(...]
    unnamed x2, local copies, waits for them, and re-layouts: 3.96 us -> 1.67 us
where the time goes in v3:
time: 75.4 us; the launch traced here: 74.9 us
  Pallas kernels  72.6 us (96%)
  local copies, waits for them, and re-layouts  1.67 us (2%)
    pallas_call x1, Pallas kernels, fused(): pl.pallas_call(functools.partial(fused_kernel, n), out_shape=(pltpu.VMEM(...  72.6 us
    unnamed x2, local copies, waits for them, and re-layouts  1.67 us

profile of v3, /device:TPU:3, one launch (start us, length us, event | category | flops | bytes accessed | tf_op | source)
XLA Modules:
  0.0 74.9 jit_solution(13405658195420531589)
XLA Ops:
  0.6 72.6 %shard_map.86 = (bf16[1,4,128,640]{3,2,1,0:T(8,128)(2,1)S(1)}, bf16[1,4,128,640]{3,2,1,0:T(8,128)(2,1)S(1)}) custom-call(bf16[1,4,128,640]{3,2,1,0:T(8,128)(2,1)} %lat.1, bf16[1,4,128,640]{3,2,1,0:T(8,128)(2,1)} %tan.1, f32[640]{0:T(1024)} %gain_a.1, f32[640]{0:T(1024)} %gain_b.1, bf16[9,160,640]{2,1,0:T(8,128)(2,1)} %bitcast.2, ...), custom_call_target="tpu_custom_call" | custom-call | tf_op jit(solution)/shard_map/pallas_call | solution.py:420
  73.2 0.8 %copy.11 = bf16[1,4,128,640]{3,2,1,0:T(8,128)(2,1)} copy(bf16[1,4,128,640]{3,2,1,0:T(8,128)(2,1)S(1)} %get-tuple-element.2) | data formatting | bytes 1310720
  74.0 0.8 %copy.12 = bf16[1,4,128,640]{3,2,1,0:T(8,128)(2,1)} copy(bf16[1,4,128,640]{3,2,1,0:T(8,128)(2,1)S(1)} %get-tuple-element.3) | data formatting | bytes 1310720

commit v4 on v3

--- a/solution.py
+++ b/solution.py
@@ -333,9 +333,14 @@
             accumulate(v, 1 + p // 2, 1 - p // 2, rows - 1)
         loop(low, high, one)
 
-    def edge(v):
-        p = tap_of(v)[0]
-        accumulate(v, (p // 2) * (rows + 1), (p // 2) * (rows - 1), 1)
+    def edge(*taps):
+        low = tap_of(taps[0])[0] // 2
+        src = pl.ds(pl.multiple_of(low * (rows + 1) * pair, 128), pair)
+        at = pl.ds(pl.multiple_of(low * (rows - 1) * pair, 128), pair)
+        acc[at] += lax.dot_general(
+            jnp.concatenate([shifted[tap_of(v)[1], src] for v in taps], axis=1),
+            jnp.concatenate([full[v] for v in taps], axis=1),
+            (((1,), (1,)), ((), ())), preferred_element_type=F32)
 
     loads[0].wait()
     loads[1].wait()
@@ -359,7 +364,8 @@
     tick(11)
     halo_wait(field, 0)
     activate_halo(field, coef)
-    loop(3, TAPS, edge)
+    edge(3, 4, 5)
+    edge(6, 7, 8)
 
     for c in loads[5:]:
         c.wait()
@@ -381,7 +387,8 @@
     inner(TAPS + 3, 17, 5)
     halo_wait(mid, 1)
     activate_halo(mid, coef)
-    loop(TAPS + 3, 17, edge)
+    edge(12, 13, 14)
+    edge(15, 16)
     tick(22)
     arrive(steps - 1)
     accumulate(steps - 1, 2, 0, rows)

time: 75.4 us -> 74.4 us (0.987)
  no operation moved by 1% of the time
where the time goes in v4:
time: 74.4 us; the launch traced here: 74.2 us
  Pallas kernels  71.9 us (97%)
  local copies, waits for them, and re-layouts  1.67 us (2%)
    pallas_call x1, Pallas kernels, fused(): pl.pallas_call(functools.partial(fused_kernel, n), out_shape=(pltpu.VMEM(...  71.9 us
    unnamed x2, local copies, waits for them, and re-layouts  1.67 us

profile of v4, /device:TPU:3, one launch (start us, length us, event | category | flops | bytes accessed | tf_op | source)
XLA Modules:
  0.0 74.2 jit_solution(16731502417468677693)
XLA Ops:
  0.6 71.9 %shard_map.86 = (bf16[1,4,128,640]{3,2,1,0:T(8,128)(2,1)S(1)}, bf16[1,4,128,640]{3,2,1,0:T(8,128)(2,1)S(1)}) custom-call(bf16[1,4,128,640]{3,2,1,0:T(8,128)(2,1)} %lat.1, bf16[1,4,128,640]{3,2,1,0:T(8,128)(2,1)} %tan.1, f32[640]{0:T(1024)} %gain_a.1, f32[640]{0:T(1024)} %gain_b.1, bf16[9,160,640]{2,1,0:T(8,128)(2,1)} %bitcast.2, ...), custom_call_target="tpu_custom_call" | custom-call | tf_op jit(solution)/shard_map/pallas_call | solution.py:427
  72.5 0.8 %copy.11 = bf16[1,4,128,640]{3,2,1,0:T(8,128)(2,1)} copy(bf16[1,4,128,640]{3,2,1,0:T(8,128)(2,1)S(1)} %get-tuple-element.2) | data formatting | bytes 1310720
  73.4 0.8 %copy.12 = bf16[1,4,128,640]{3,2,1,0:T(8,128)(2,1)} copy(bf16[1,4,128,640]{3,2,1,0:T(8,128)(2,1)S(1)} %get-tuple-element.3) | data formatting | bytes 1310720
